TPU v7x, 32 devices: a whole 2x2x4 slice. The times are simulated.
32 devices in a mesh: kv: 16 (over z, x, core), tp: 2 (over y).
Axes of the slice: x: 2, y: 2, z: 4, core: 2. Of those that a mesh axis runs over, the one named last changes fastest.
Arguments:
- queries: bfloat16 [16, 128, 576], P(None, 'tp'), may hold values from -36 to 36
- cache: bfloat16 [16, 4096, 576], P(None, 'kv'), may hold values from -6 to 6
- lengths: int32 [16], replicated, may hold values from 1 to 4096, as said below
- w_ov: bfloat16 [128, 512, 7168], P('tp', None, 'kv'), may hold values from -0.0234375 to 0.0234375
- resid: bfloat16 [16, 7168], P(None, 'tp'), may hold values from -3 to 3
- gain: float32 [7168], P('tp'), may hold values from 0.5 to 1.5
- w_gate: bfloat16 [7168, 18432], P('tp', 'kv'), may hold values from -0.0625 to 0.0625
- w_up: bfloat16 [7168, 18432], P('tp', 'kv'), may hold values from -0.0625 to 0.0625
- w_down: bfloat16 [18432, 7168], P('kv', 'tp'), may hold values from -0.046875 to 0.046875
Outputs:
- layer_out: bfloat16 [16, 7168], P(None, 'tp')
Inputs may be any that keep to these rules, and one draw needn't show every extreme that they name: Sequence b attends to positions 0 to lengths[b] - 1; in every draw some sequence has all 4096 positions live.
All inputs are finite; a program needn't handle non-finite values.
Results may differ from a plain program's by a relative error of at most 0.006.
Values sent between devices are 32-bit elements; how exact they have to be, the bound alone decides.
A program may use at most 128 MiB of HBM per device.

v0:
```python
import jax
import jax.numpy as jnp
from jax import lax
from jax.sharding import PartitionSpec as P

D = 7168
LAT = 512
softmax_scale = 192.0 ** (-0.5)
masked_score = -1e30
norm_floor = 0.05


def per_device(queries, cache, lengths, w_ov, resid, gain, w_gate, w_up, w_down):
    rows = cache.shape[1]
    first_row = lax.axis_index("kv") * rows
    place = first_row + lax.iota(jnp.int32, rows)
    live = (place[None, :] < lengths[:, None])[:, None, :]
    scores = (
        jnp.einsum("bhc,brc->bhr", queries, cache, preferred_element_type=jnp.float32)
        * softmax_scale
    )
    scores = jnp.where(live, scores, masked_score)
    peak = jnp.max(scores, axis=2)
    weights = jnp.where(live, jnp.exp(scores - peak[:, :, None]), 0.0)
    total = jnp.sum(weights, axis=2)
    mixed = jnp.einsum(
        "bhr,brc->bhc",
        weights.astype(jnp.bfloat16),
        cache[:, :, :LAT],
        preferred_element_type=jnp.float32,
    )
    top = lax.pmax(peak, "kv")
    factor = jnp.exp(peak - top)
    total, mixed = lax.psum((total * factor, mixed * factor[:, :, None]), "kv")
    heads_out = mixed / total[:, :, None]
    attn_part = jnp.einsum(
        "bhc,hcd->bd", heads_out.astype(jnp.bfloat16), w_ov, preferred_element_type=jnp.float32
    )
    partial_rows = lax.all_gather(attn_part, "kv", axis=1, tiled=True)
    attn = lax.psum_scatter(partial_rows, "tp", scatter_dimension=1, tiled=True)
    state = resid.astype(jnp.float32) + attn
    squares = lax.psum(jnp.sum(state * state, axis=1), "tp")
    scaled = (state * lax.rsqrt(squares / D + norm_floor)[:, None] * gain[None, :]).astype(
        jnp.bfloat16
    )
    gate_part = jnp.dot(scaled, w_gate, preferred_element_type=jnp.float32)
    up_part = jnp.dot(scaled, w_up, preferred_element_type=jnp.float32)
    gate, up = lax.psum((gate_part, up_part), "tp")
    inner = (jax.nn.silu(gate) * up).astype(jnp.bfloat16)
    ffn = lax.psum(jnp.dot(inner, w_down, preferred_element_type=jnp.float32), "kv")
    return (state + ffn).astype(jnp.bfloat16)


def solution(mesh):
    in_specs = (
        P(None, "tp", None),
        P(None, "kv", None),
        P(),
        P("tp", None, "kv"),
        P(None, "tp"),
        P("tp"),
        P("tp", "kv"),
        P("tp", "kv"),
        P("kv", "tp"),
    )
    out_specs = P(None, "tp")
    return jax.shard_map(
        per_device, mesh=mesh, in_specs=in_specs, out_specs=out_specs, check_vma=False
    )
```

profile of v0, /device:TPU:8, one launch (start us, length us, event | category | flops | bytes accessed | tf_op | source)
XLA Modules:
  0.0 339.4 jit_solution(5535327075866248540)
XLA Ops:
  6.5 0.0 copy-start
  6.5 0.0 all-reduce.5.cloned.1.call-start
  6.5 0.8 broadcast_compare_fusion
  7.4 0.5 copy-done
  7.9 3.4 fusion.18
  11.3 25.9 %pmax.7 = f32[16,64]{1,0:T(8,128)S(1)} all-reduce(f32[16,64]{1,0:T(8,128)S(1)} %get-tuple-element.9), channel_id=1, replica_groups=mesh['kv'=16,'tp'=2] {'kv'}, use_global_device_ids=true, to_apply=%region_1.2 | all-reduce | flops 1024 | bytes 8192 | tf_op jit(solution)/shard_map/pmax | solution.py:32
  37.2 0.4 fusion.7
  37.6 4.9 %fusion.2 = f32[16,64,512]{2,1,0:T(8,128)} fusion(bf16[16,256,576]{1,2,0:T(8,128)(2,1)} %param.10, f32[16,64]{1,0:T(8,128)S(1)} %get-tuple-element.8, f32[16,64,256]{2,1,0:T(8,128)S(1)} %get-tuple-element.10, f32[16,64]{1,0:T(8,128)S(1)} %get-tuple-element.9, pred[16,256]{1,0:T(8,128)(4,1)S(1)} %broadcast_compare_fusion), kind=kOutput, calls=%fused_computation.3 | convolution fusion | flops 269746176 | bytes 7352320 | tf_op jit(solution)/shard_map/bhr,brc->bhc/dot_general | solution.py:26
  42.5 0.0 all-reduce.5.cloned.1.call-update
  42.5 0.0 reduce-scatter.2.cloned.1.call-start
  42.6 30.3 %psum.43 = f32[16,64]{1,0:T(8,128)S(1)} all-reduce(f32[16,64]{1,0:T(8,128)S(1)} %get-tuple-element.7), channel_id=1, replica_groups=mesh['kv'=16,'tp'=2] {'kv'}, use_global_device_ids=true, to_apply=%region_4.5 | all-reduce | flops 1024 | bytes 8192 | tf_op jit(solution)/shard_map/psum | solution.py:34
  72.8 73.7 %all-reduce.5.cloned.1.call-done = f32[16,64,512]{2,1,0:T(8,128)} async-done(((f32[16,64,512]{2,1,0:T(8,128)}), f32[16,64,512]{2,1,0:T(8,128)}) %all-reduce.5.cloned.1.call-update) | async-done | bytes 2097168 | tf_op jit(solution)/shard_map/psum | solution.py:34
  146.5 1.8 divide_convert_fusion
  148.3 0.0 copy-start.3
  148.3 0.0 copy-start.4
  148.3 13.3 %convolution_bitcast_fusion = f32[1,448,16]{1,2,0:T(8,128)S(1)} fusion(bf16[64,512,448]{1,2,0:T(8,128)(2,1)} %param.12, bf16[16,64,512]{2,1,0:T(8,128)(2,1)S(1)} %divide_convert_fusion), kind=kOutput, calls=%fused_computation.6 | convolution fusion | flops 469762048 | bytes 30437376 | tf_op jit(solution)/shard_map/bhc,hcd->bd/dot_general | solution.py:36
  161.6 18.3 %all-gather = f32[16,448,16]{1,2,0:T(8,128)S(1)} all-gather(f32[1,448,16]{1,2,0:T(8,128)S(1)} %convolution_bitcast_fusion), channel_id=1, replica_groups=mesh['kv'=16,'tp'=2] {'kv'}, dimensions={0}, use_global_device_ids=true | all-gather | bytes 487424 | tf_op jit(solution)/shard_map/all_gather | solution.py:39
  179.9 0.3 copy.17
  180.2 1.0 reshape.33
  181.2 0.0 reduce-scatter.2.cloned.1.call-update
  181.2 0.0 all-reduce.9.cloned.1.call-start
  181.3 14.0 %reduce-scatter.2.cloned.1.call-done = f32[16,3584]{1,0:T(8,128)} async-done(((f32[16,7168]{1,0:T(8,128)}), f32[16,3584]{1,0:T(8,128)}) %reduce-scatter.2.cloned.1.call-update) | async-done | bytes 229392 | tf_op jit(solution)/shard_map/reduce_scatter | solution.py:40
  195.3 0.0 copy-done.3
  195.3 1.1 multiply_reduce_fusion
  196.3 4.9 %psum.44 = f32[16]{0:T(128)S(1)} all-reduce(f32[16]{0:T(128)S(1)} %multiply_reduce_fusion), channel_id=1, replica_groups=mesh['kv'=16,'tp'=2] {'tp'}, use_global_device_ids=true, to_apply=%region_7.8 | all-reduce | flops 16 | bytes 128 | tf_op jit(solution)/shard_map/psum | solution.py:42
  201.3 0.0 copy-done.4
  201.3 1.0 multiply_convert_fusion
  202.3 5.2 %fusion.20 = f32[16,1152]{1,0:T(8,128)} fusion(bf16[16,3584]{1,0:T(8,128)(2,1)S(1)} %multiply_convert_fusion, bf16[3584,1152]{1,0:T(8,128)(2,1)} %param.16), kind=kOutput, calls=%fused_computation.30 | convolution fusion | flops 132120576 | bytes 8445952 | tf_op jit(solution)/shard_map/dot_general | solution.py:47
  207.5 5.1 %fusion.19 = f32[16,1152]{1,0:T(8,128)} fusion(bf16[16,3584]{1,0:T(8,128)(2,1)S(1)} %multiply_convert_fusion, bf16[3584,1152]{1,0:T(8,128)(2,1)} %param.15), kind=kOutput, calls=%fused_computation.29 | convolution fusion | flops 132120576 | bytes 8445952 | tf_op jit(solution)/shard_map/dot_general | solution.py:46
  212.6 0.0 all-reduce.9.cloned.1.call-update
  212.6 0.0 all-reduce.7.cloned.1.call-start
  212.7 21.9 %all-reduce.9.cloned.1.call-done = (f32[16,1152]{1,0:T(8,128)}, f32[16,1152]{1,0:T(8,128)}) async-done(((f32[16,1152]{1,0:T(8,128)}, f32[16,1152]{1,0:T(8,128)}), (f32[16,1152]{1,0:T(8,128)}, f32[16,1152]{1,0:T(8,128)})) %all-reduce.9.cloned.1.call-update) | async-done | bytes 147472 | tf_op jit(solution)/shard_map/psum | solution.py:48
  234.6 0.0 copy-start.1
  234.6 0.0 copy-start.2
  234.6 5.4 %fusion.13 = f32[16,3584]{1,0:T(8,128)} fusion(bf16[1152,3584]{1,0:T(8,128)(2,1)} %param.17, f32[16,1152]{1,0:T(8,128)} %get-tuple-element.5, f32[16,1152]{1,0:T(8,128)} %get-tuple-element.6), kind=kOutput, calls=%fused_computation.19 | convolution fusion | flops 132231168 | bytes 8634368 | tf_op jit(solution)/shard_map/dot_general | solution.py:50
  240.0 0.0 all-reduce.7.cloned.1.call-update
  240.0 91.2 %all-reduce.7.cloned.1.call-done = f32[16,3584]{1,0:T(8,128)} async-done(((f32[16,3584]{1,0:T(8,128)}), f32[16,3584]{1,0:T(8,128)}) %all-reduce.7.cloned.1.call-update) | async-done | bytes 229392 | tf_op jit(solution)/shard_map/psum | solution.py:50
  331.2 0.0 copy-done.2
  331.3 1.6 add_convert_fusion
  332.9 0.0 copy-done.1
  (3 shorter events, 0.0 us)
Async XLA Ops:
  6.5 1.3 copy-start
  6.5 140.0 %all-reduce.5.cloned.1.call-start = ((), (), s32[]{:S(2)}) async-start(), calls=%async_computation.1 | async-start | bytes 4194304 | tf_op jit(solution)/shard_map/psum | solution.py:34
  42.5 152.7 %reduce-scatter.2.cloned.1.call-start = ((), (), s32[]{:S(2)}) async-start(), calls=%async_computation.2 | async-start | bytes 688128 | tf_op jit(solution)/shard_map/reduce_scatter | solution.py:40
  148.3 46.9 %copy-start.3 = (bf16[16,3584]{1,0:T(8,128)(2,1)S(1)}, bf16[16,3584]{1,0:T(8,128)(2,1)}, u32[]{:S(2)}) copy-start(bf16[16,3584]{1,0:T(8,128)(2,1)} %param.13) | copy-start | bytes 344068
  148.3 53.0 %copy-start.4 = (f32[3584]{0:T(1024)S(1)}, f32[3584]{0:T(1024)}, u32[]{:S(2)}) copy-start(f32[3584]{0:T(1024)} %param.14) | copy-start | bytes 43012
  181.2 53.3 %all-reduce.9.cloned.1.call-start = ((), (), s32[]{:S(2)}) async-start(), calls=%async_computation.4 | async-start | bytes 294912 | tf_op jit(solution)/shard_map/psum | solution.py:48
  212.6 118.6 %all-reduce.7.cloned.1.call-start = ((), (), s32[]{:S(2)}) async-start(), calls=%async_computation.3 | async-start | bytes 458752 | tf_op jit(solution)/shard_map/psum | solution.py:50
  234.6 98.3 %copy-start.1 = (bf16[16,64,576]{2,1,0:T(8,128)(2,1)S(1)}, bf16[16,64,576]{2,1,0:T(8,128)(2,1)}, u32[]{:S(2)}) copy-start(bf16[16,64,576]{2,1,0:T(8,128)(2,1)} %param.9) | copy-start | bytes 3538948
  234.6 96.7 %copy-start.2 = (f32[16,3584]{1,0:T(8,128)S(1)}, f32[16,3584]{1,0:T(8,128)}, u32[]{:S(2)}) copy-start(f32[16,3584]{1,0:T(8,128)} %reduce-scatter.2.cloned.1.call-done) | copy-start | bytes 688132
Sparse Core Ops, SparseCore 0:
  42.6 103.8 all-reduce.4
  181.4 13.8 reduce-scatter.1
  212.8 21.7 all-reduce.8
  240.1 91.0 all-reduce.6
where the time goes:
time: 340 us; the launch traced here: 339 us
  waiting for transfers between devices  201 us (59%)
  blocking collectives  79.4 us (23%)
  matrix products  37.3 us (11%)
  between operations  13.2 us (4%)
  other arithmetic  6.8 us (2%)
    psum x1, waiting for transfers between devices, per_device(): lax.psum(jnp.dot(inner, w_down, preferred_element_type=jnp.float32), 'kv')  91.2 us
    psum x1, waiting for transfers between devices, per_device(): total, mixed = lax.psum((total * factor, mixed * factor[:, :, None]), 'kv')  73.7 us
    psum x1, blocking collectives, per_device(): total, mixed = lax.psum((total * factor, mixed * factor[:, :, None]), 'kv')  30.3 us
    pmax x1, blocking collectives, per_device(): top = lax.pmax(peak, 'kv')  25.9 us
    psum x1, waiting for transfers between devices, per_device(): gate, up = lax.psum((gate_part, up_part), 'tp')  21.9 us
    all_gather x1, blocking collectives, per_device(): partial_rows = lax.all_gather(attn_part, 'kv', axis=1, tiled=True)  18.3 us
    reduce_scatter x1, waiting for transfers between devices, per_device(): attn = lax.psum_scatter(partial_rows, 'tp', scatter_dimension=1, tiled=True)  14 us
    dot_general x1, matrix products, per_device(): jnp.einsum('bhc,hcd->bd', heads_out.astype(jnp.bfloat16), w_ov, preferred...  13.3 us
  transfers between devices with their start and end apart: 4, of which 4 were waited for; matrix products, arithmetic and copies ran while one was open for 0% of the time, Pallas kernels for 0%

commit v1 on v0

--- a/solution.py
+++ b/solution.py
@@ -8,6 +8,12 @@
 softmax_scale = 192.0 ** (-0.5)
 masked_score = -1e30
 norm_floor = 0.05
+
+
+def add_all(x, axis):
+    pieces = lax.all_gather(x, axis, axis=0, tiled=False)
+    acc = pieces.sum(axis=0)
+    return acc
 
 
 def per_device(queries, cache, lengths, w_ov, resid, gain, w_gate, w_up, w_down):
@@ -47,7 +53,7 @@
     up_part = jnp.dot(scaled, w_up, preferred_element_type=jnp.float32)
     gate, up = lax.psum((gate_part, up_part), "tp")
     inner = (jax.nn.silu(gate) * up).astype(jnp.bfloat16)
-    ffn = lax.psum(jnp.dot(inner, w_down, preferred_element_type=jnp.float32), "kv")
+    ffn = add_all(jnp.dot(inner, w_down, preferred_element_type=jnp.float32), "kv")
     return (state + ffn).astype(jnp.bfloat16)
 
 

time: 340 us -> 299 us (0.88)
  waiting for transfers between devices: 201 us -> 158 us
    psum x1 -> x0, waiting for transfers between devices: 91.2 us -> none  [per_device(): lax.psum(jnp.dot(inner, w_down, preferred_element_type=jnp.float32), 'kv')]
    all_gather x0 -> x1, waiting for transfers between devices: none -> 48.1 us  [add_all(): pieces = lax.all_gather(x, axis, axis=0, tiled=False)]
where the time goes in v1:
time: 299 us; the launch traced here: 298 us
  waiting for transfers between devices  158 us (53%)
  blocking collectives  79.4 us (27%)
  matrix products  37.3 us (12%)
  between operations  13.2 us (4%)
  other arithmetic  8.09 us (3%)
    psum x1, waiting for transfers between devices, per_device(): total, mixed = lax.psum((total * factor, mixed * factor[:, :, None]), 'kv')  73.7 us
    all_gather x1, waiting for transfers between devices, add_all(): pieces = lax.all_gather(x, axis, axis=0, tiled=False)  48.1 us
    psum x1, blocking collectives, per_device(): total, mixed = lax.psum((total * factor, mixed * factor[:, :, None]), 'kv')  30.3 us
    pmax x1, blocking collectives, per_device(): top = lax.pmax(peak, 'kv')  25.9 us
    psum x1, waiting for transfers between devices, per_device(): gate, up = lax.psum((gate_part, up_part), 'tp')  21.9 us
    all_gather x1, blocking collectives, per_device(): partial_rows = lax.all_gather(attn_part, 'kv', axis=1, tiled=True)  18.3 us
    reduce_scatter x1, waiting for transfers between devices, per_device(): attn = lax.psum_scatter(partial_rows, 'tp', scatter_dimension=1, tiled=True)  14 us
    dot_general x1, matrix products, per_device(): jnp.einsum('bhc,hcd->bd', heads_out.astype(jnp.bfloat16), w_ov, preferred...  13.3 us
  transfers between devices with their start and end apart: 4, of which 4 were waited for; matrix products, arithmetic and copies ran while one was open for 0% of the time, Pallas kernels for 0%

profile of v1, /device:TPU:8, one launch (start us, length us, event | category | flops | bytes accessed | tf_op | source)
XLA Modules:
  0.0 297.6 jit_solution(11099253766993231095)
XLA Ops:
  6.5 0.0 copy-start
  6.5 0.0 all-reduce.4.cloned.1.call-start
  6.5 0.8 broadcast_compare_fusion
  7.4 0.5 copy-done
  7.9 3.4 %fusion.18 = (f32[16,64]{1,0:T(8,128)S(1)}, f32[16,64,256]{2,1,0:T(8,128)S(1)}) fusion(bf16[16,64,576]{2,1,0:T(8,128)(2,1)S(1)} %copy-done, bf16[16,256,576]{1,2,0:T(8,128)(2,1)} %param.10, pred[16,256]{1,0:T(8,128)(4,1)S(1)} %broadcast_compare_fusion), kind=kOutput, calls=%fused_computation.28 | convolution fusion | flops 302775296 | bytes 6955008 | tf_op jit(solution)/shard_map/bhc,brc->bhr/dot_general | solution.py:25
  11.3 25.9 %pmax.7 = f32[16,64]{1,0:T(8,128)S(1)} all-reduce(f32[16,64]{1,0:T(8,128)S(1)} %get-tuple-element.9), channel_id=1, replica_groups=mesh['kv'=16,'tp'=2] {'kv'}, use_global_device_ids=true, to_apply=%region_1.2 | all-reduce | flops 1024 | bytes 8192 | tf_op jit(solution)/shard_map/pmax | solution.py:38
  37.2 0.4 fusion.7
  37.6 4.9 %fusion.2 = f32[16,64,512]{2,1,0:T(8,128)} fusion(bf16[16,256,576]{1,2,0:T(8,128)(2,1)} %param.10, f32[16,64]{1,0:T(8,128)S(1)} %get-tuple-element.8, f32[16,64,256]{2,1,0:T(8,128)S(1)} %get-tuple-element.10, f32[16,64]{1,0:T(8,128)S(1)} %get-tuple-element.9, pred[16,256]{1,0:T(8,128)(4,1)S(1)} %broadcast_compare_fusion), kind=kOutput, calls=%fused_computation.3 | convolution fusion | flops 269746176 | bytes 7352320 | tf_op jit(solution)/shard_map/bhr,brc->bhc/dot_general | solution.py:32
  42.5 0.0 all-reduce.4.cloned.1.call-update
  42.5 0.0 reduce-scatter.2.cloned.1.call-start
  42.6 30.3 %psum.36 = f32[16,64]{1,0:T(8,128)S(1)} all-reduce(f32[16,64]{1,0:T(8,128)S(1)} %get-tuple-element.7), channel_id=1, replica_groups=mesh['kv'=16,'tp'=2] {'kv'}, use_global_device_ids=true, to_apply=%region_4.5 | all-reduce | flops 1024 | bytes 8192 | tf_op jit(solution)/shard_map/psum | solution.py:40
  72.8 73.7 %all-reduce.4.cloned.1.call-done = f32[16,64,512]{2,1,0:T(8,128)} async-done(((f32[16,64,512]{2,1,0:T(8,128)}), f32[16,64,512]{2,1,0:T(8,128)}) %all-reduce.4.cloned.1.call-update) | async-done | bytes 2097168 | tf_op jit(solution)/shard_map/psum | solution.py:40
  146.5 1.8 divide_convert_fusion
  148.3 0.0 copy-start.3
  148.3 0.0 copy-start.4
  148.3 13.3 %convolution_bitcast_fusion = f32[1,448,16]{1,2,0:T(8,128)S(1)} fusion(bf16[64,512,448]{1,2,0:T(8,128)(2,1)} %param.12, bf16[16,64,512]{2,1,0:T(8,128)(2,1)S(1)} %divide_convert_fusion), kind=kOutput, calls=%fused_computation.6 | convolution fusion | flops 469762048 | bytes 30437376 | tf_op jit(solution)/shard_map/bhc,hcd->bd/dot_general | solution.py:42
  161.6 18.3 %all-gather.1 = f32[16,448,16]{1,2,0:T(8,128)S(1)} all-gather(f32[1,448,16]{1,2,0:T(8,128)S(1)} %convolution_bitcast_fusion), channel_id=1, replica_groups=mesh['kv'=16,'tp'=2] {'kv'}, dimensions={0}, use_global_device_ids=true | all-gather | bytes 487424 | tf_op jit(solution)/shard_map/all_gather | solution.py:45
  179.9 0.3 copy.17
  180.2 1.0 reshape.34
  181.2 0.0 reduce-scatter.2.cloned.1.call-update
  181.2 0.0 all-reduce.6.cloned.1.call-start
  181.3 14.0 %reduce-scatter.2.cloned.1.call-done = f32[16,3584]{1,0:T(8,128)} async-done(((f32[16,7168]{1,0:T(8,128)}), f32[16,3584]{1,0:T(8,128)}) %reduce-scatter.2.cloned.1.call-update) | async-done | bytes 229392 | tf_op jit(solution)/shard_map/reduce_scatter | solution.py:46
  195.3 0.0 copy-done.3
  195.3 1.1 multiply_reduce_fusion
  196.3 4.9 %psum.37 = f32[16]{0:T(128)S(1)} all-reduce(f32[16]{0:T(128)S(1)} %multiply_reduce_fusion), channel_id=1, replica_groups=mesh['kv'=16,'tp'=2] {'tp'}, use_global_device_ids=true, to_apply=%region_7.8 | all-reduce | flops 16 | bytes 128 | tf_op jit(solution)/shard_map/psum | solution.py:48
  201.3 0.0 copy-done.4
  201.3 1.0 multiply_convert_fusion
  202.3 5.2 %fusion.20 = f32[16,1152]{1,0:T(8,128)} fusion(bf16[16,3584]{1,0:T(8,128)(2,1)S(1)} %multiply_convert_fusion, bf16[3584,1152]{1,0:T(8,128)(2,1)} %param.16), kind=kOutput, calls=%fused_computation.30 | convolution fusion | flops 132120576 | bytes 8445952 | tf_op jit(solution)/shard_map/dot_general | solution.py:53
  207.5 5.2 %fusion.19 = f32[16,1152]{1,0:T(8,128)} fusion(bf16[16,3584]{1,0:T(8,128)(2,1)S(1)} %multiply_convert_fusion, bf16[3584,1152]{1,0:T(8,128)(2,1)} %param.15), kind=kOutput, calls=%fused_computation.29 | convolution fusion | flops 132120576 | bytes 8445952 | tf_op jit(solution)/shard_map/dot_general | solution.py:52
  212.6 0.0 all-reduce.6.cloned.1.call-update
  212.7 0.0 all-gather.4.cloned.1.call-start
  212.7 21.9 %all-reduce.6.cloned.1.call-done = (f32[16,1152]{1,0:T(8,128)}, f32[16,1152]{1,0:T(8,128)}) async-done(((f32[16,1152]{1,0:T(8,128)}, f32[16,1152]{1,0:T(8,128)}), (f32[16,1152]{1,0:T(8,128)}, f32[16,1152]{1,0:T(8,128)})) %all-reduce.6.cloned.1.call-update) | async-done | bytes 147472 | tf_op jit(solution)/shard_map/psum | solution.py:54
  234.6 0.0 copy-start.2
  234.6 0.0 copy-start.1
  234.6 5.4 %fusion.13 = f32[16,3584]{1,0:T(8,128)} fusion(bf16[1152,3584]{1,0:T(8,128)(2,1)} %param.17, f32[16,1152]{1,0:T(8,128)} %get-tuple-element.5, f32[16,1152]{1,0:T(8,128)} %get-tuple-element.6), kind=kOutput, calls=%fused_computation.19 | convolution fusion | flops 132231168 | bytes 8634368 | tf_op jit(solution)/shard_map/dot_general | solution.py:56
  240.0 0.0 all-gather.4.cloned.1.call-update
  240.0 48.1 %all-gather.4.cloned.1.call-done = f32[256,3584]{1,0:T(8,128)} async-done(((f32[16,3584]{1,0:T(8,128)}), f32[256,3584]{1,0:T(8,128)}) %all-gather.4.cloned.1.call-update) | async-done | bytes 3670032 | tf_op jit(solution)/shard_map/all_gather | solution.py:14
  288.1 2.2 reduce_sum.29
  290.3 0.0 copy-done.2
  290.3 0.7 add_convert_fusion
  291.0 0.0 copy-done.1
  (3 shorter events, 0.0 us)
Async XLA Ops:
  6.5 1.3 copy-start
  6.5 140.0 %all-reduce.4.cloned.1.call-start = ((), (), s32[]{:S(2)}) async-start(), calls=%async_computation.1 | async-start | bytes 4194304 | tf_op jit(solution)/shard_map/psum | solution.py:40
  42.5 152.7 %reduce-scatter.2.cloned.1.call-start = ((), (), s32[]{:S(2)}) async-start(), calls=%async_computation.2 | async-start | bytes 688128 | tf_op jit(solution)/shard_map/reduce_scatter | solution.py:46
  148.3 46.9 %copy-start.3 = (bf16[16,3584]{1,0:T(8,128)(2,1)S(1)}, bf16[16,3584]{1,0:T(8,128)(2,1)}, u32[]{:S(2)}) copy-start(bf16[16,3584]{1,0:T(8,128)(2,1)} %param.13) | copy-start | bytes 344068
  148.3 53.0 %copy-start.4 = (f32[3584]{0:T(1024)S(1)}, f32[3584]{0:T(1024)}, u32[]{:S(2)}) copy-start(f32[3584]{0:T(1024)} %param.14) | copy-start | bytes 43012
  181.2 53.4 %all-reduce.6.cloned.1.call-start = ((), (), s32[]{:S(2)}) async-start(), calls=%async_computation.4 | async-start | bytes 294912 | tf_op jit(solution)/shard_map/psum | solution.py:54
  212.7 75.4 %all-gather.4.cloned.1.call-start = ((), (), s32[]{:S(2)}) async-start(), calls=%async_computation.3 | async-start | bytes 3899392 | tf_op jit(solution)/shard_map/all_gather | solution.py:14
  234.6 55.7 %copy-start.2 = (f32[16,3584]{1,0:T(8,128)S(1)}, f32[16,3584]{1,0:T(8,128)}, u32[]{:S(2)}) copy-start(f32[16,3584]{1,0:T(8,128)} %reduce-scatter.2.cloned.1.call-done) | copy-start | bytes 688132
  234.6 56.4 %copy-start.1 = (bf16[16,64,576]{2,1,0:T(8,128)(2,1)S(1)}, bf16[16,64,576]{2,1,0:T(8,128)(2,1)}, u32[]{:S(2)}) copy-start(bf16[16,64,576]{2,1,0:T(8,128)(2,1)} %param.9) | copy-start | bytes 3538948
Sparse Core Ops, SparseCore 0:
  42.6 103.8 all-reduce.3
  181.4 13.8 reduce-scatter.1
  212.8 21.7 all-reduce.5
  240.2 47.8 all-gather.3
